TPU v7x, 32 devices: a whole 2x2x4 slice. The times are simulated.
32 devices in a mesh: grp: 2 (over y), ctx: 4 (over z), hd: 4 (over x, core).
Axes of the slice: x: 2, y: 2, z: 4, core: 2. Of those that a mesh axis runs over, the one named last changes fastest.
Arguments:
- query: bfloat16 [1024, 4096], P(('grp', 'ctx'), 'hd'), parts along dimension 0, may hold values from -6 to 6
- keys: bfloat16 [1024, 1024], P(('grp', 'ctx'), 'hd'), parts along dimension 0, may hold values from -6 to 6
- values: bfloat16 [1024, 1024], P(('grp', 'ctx'), 'hd'), parts along dimension 0, may hold values from -6 to 6
- m_x: bfloat16 [1024, 8192], P(('grp', 'ctx'), 'hd'), parts along dimension 0, may hold values from -6 to 6
- m_z: bfloat16 [1024, 8192], P(('grp', 'ctx'), 'hd'), parts along dimension 0, may hold values from -6 to 6
- m_b: bfloat16 [1024, 1024], P(('grp', 'ctx'), 'hd'), parts along dimension 0, may hold values from -6 to 6
- m_c: bfloat16 [1024, 1024], P(('grp', 'ctx'), 'hd'), parts along dimension 0, may hold values from -0.5 to 0.5
- dt_raw: bfloat16 [1024, 128], P(('grp', 'ctx'), 'hd'), parts along dimension 0, may hold values from -5 to 25
- dt_bias: float32 [128], P('hd'), may hold values from -0.5 to 0.5
- a_log: float32 [128], P('hd'), may hold values from -10 to 0
- d_skip: float32 [128], P('hd'), may hold values from 0.5 to 2
- norm_gain: float32 [8192], P('hd'), may hold values from 0.5 to 1.5
Outputs:
- context: bfloat16 [1024, 4096], P(('grp', 'ctx'), 'hd'), parts along dimension 0
- mixed: bfloat16 [1024, 8192], P(('grp', 'ctx'), 'hd'), parts along dimension 0
There are 2 independent parts, one for each index of `grp`. A program takes and returns all parts, laid end to end along the dimension named above; an argument that names none is the same for every part. Nothing has to cross between parts.
All inputs are finite; a program needn't handle non-finite values.
Results may differ from a plain program's by a relative error of at most 0.009.
Values may be sent and summed in bfloat16 or wider, within the bound.
A program may use at most 64 MiB of HBM per device.

v0:
```python
import math
import jax
import jax.numpy as jnp
from jax import lax
from jax.sharding import PartitionSpec as P

HEAD_SIZE = 128
MP = 64
MN = 128
highest = lax.Precision.HIGHEST
norm_eps = 1e-05
masked_score = -1e30


def token_position(row_index, tok_rows, ctx_count):
    device = row_index // tok_rows
    within = row_index - device * tok_rows
    half_rows = tok_rows // 2
    second = within >= half_rows
    block_index = jnp.where(second, 2 * ctx_count - 1 - device, device)
    return block_index * half_rows + within - jnp.where(second, half_rows, 0)


def pick_block(total_rows, limit):
    selected = 1
    for candidate in range(1, min(total_rows, limit) + 1):
        if total_rows % candidate == 0:
            selected = candidate
    return selected


def folded_to_sequence(whole, ctx_count):
    half_rows = whole.shape[0] // (2 * ctx_count)
    blocks = whole.reshape((ctx_count, 2, half_rows) + whole.shape[1:])
    return jnp.concatenate([blocks[:, 0], blocks[::-1, 1]], axis=0).reshape(whole.shape)


def attend(query, keys, values):
    tok_rows = query.shape[0]
    ctx_count = lax.axis_size("ctx")
    kv_local = keys.shape[1] // HEAD_SIZE
    heads_per_group = query.shape[1] // keys.shape[1]
    query_heads = query.reshape(tok_rows, kv_local, heads_per_group, HEAD_SIZE)
    own_rows = lax.axis_index("ctx") * tok_rows + jnp.arange(tok_rows, dtype=jnp.int32)
    query_pos = token_position(own_rows, tok_rows, ctx_count)
    scaling = 1.0 / math.sqrt(HEAD_SIZE)
    start_max = jnp.full((kv_local, heads_per_group, tok_rows), masked_score, jnp.float32)
    start_sum = jnp.zeros((kv_local, heads_per_group, tok_rows), jnp.float32)
    start_acc = jnp.zeros((kv_local, heads_per_group, tok_rows, HEAD_SIZE), jnp.float32)
    start = jnp.int32(0)
    key_piece = lax.all_gather(keys, "ctx", axis=0, tiled=True)
    value_piece = lax.all_gather(values, "ctx", axis=0, tiled=True)
    piece_rows = key_piece.shape[0]
    rows_per_block = pick_block(piece_rows, 1024)

    def one_block(index, running):
        running_max, running_sum, running_acc = running
        offset = index * rows_per_block
        key_block = lax.dynamic_slice_in_dim(key_piece, offset, rows_per_block, 0).reshape(
            rows_per_block, kv_local, HEAD_SIZE
        )
        value_block = lax.dynamic_slice_in_dim(value_piece, offset, rows_per_block, 0).reshape(
            rows_per_block, kv_local, HEAD_SIZE
        )
        key_pos = token_position(
            start + offset + jnp.arange(rows_per_block, dtype=jnp.int32), tok_rows, ctx_count
        )
        visible = key_pos[None, :] <= query_pos[:, None]
        scores = (
            jnp.einsum("qhgd,khd->hgqk", query_heads, key_block, preferred_element_type=jnp.float32)
            * scaling
        )
        scores = jnp.where(visible, scores, masked_score)
        new_max = jnp.maximum(running_max, jnp.max(scores, axis=-1))
        weights = jnp.where(visible, jnp.exp(scores - new_max[..., None]), 0.0)
        factor = jnp.exp(running_max - new_max)
        new_sum = running_sum * factor + jnp.sum(weights, axis=-1)
        update = jnp.einsum(
            "hgqk,khd->hgqd",
            weights.astype(jnp.bfloat16),
            value_block,
            preferred_element_type=jnp.float32,
        )
        return (new_max, new_sum, running_acc * factor[..., None] + update)

    final_max, final_sum, final_acc = lax.fori_loop(
        0, piece_rows // rows_per_block, one_block, (start_max, start_sum, start_acc)
    )
    averaged = final_acc / final_sum[..., None]
    return jnp.transpose(averaged, (2, 0, 1, 3)).reshape(tok_rows, -1).astype(jnp.bfloat16)


def ssd_block(inputs, steps, rates, b_rows, c_rows):
    intersection = jnp.dot(c_rows, b_rows.T, preferred_element_type=jnp.float32)
    inputs = inputs.astype(jnp.float32)
    b_rows = b_rows.astype(jnp.float32)
    sequence_length = inputs.shape[0]
    running = jnp.cumsum(-steps * rates, axis=0)
    lower = jnp.arange(sequence_length)[:, None] >= jnp.arange(sequence_length)[None, :]
    spread = running[:, None, :] - running[None, :, :]
    decay = jnp.exp(jnp.where(lower[:, :, None], spread, -jnp.inf))
    weights = intersection[:, :, None] * decay * steps[None, :, :]
    inner = jnp.einsum("ijh,jhp->ihp", weights, inputs, precision=highest)
    tail_weight = jnp.exp(running[-1][None, :] - running) * steps
    state = jnp.einsum("jh,jhp,jn->hpn", tail_weight, inputs, b_rows, precision=highest)
    return (inner, state, jnp.exp(running[-1]), jnp.exp(running))


def chain_states(earlier, later):
    return (earlier[0] * later[0], earlier[1] * later[0][..., None, None] + later[1])


def ssd_sequence(inputs, steps, rates, b_rows, c_rows):
    sequence_length, head_count, width = inputs.shape
    block_len = math.gcd(sequence_length, 128)
    count = sequence_length // block_len
    c_blocks = c_rows.reshape(count, block_len, -1)
    inner, state, totals, scaled = jax.vmap(ssd_block, in_axes=(0, 0, None, 0, 0))(
        inputs.reshape(count, block_len, head_count, width),
        steps.reshape(count, block_len, head_count),
        rates,
        b_rows.reshape(count, block_len, -1),
        c_blocks,
    )
    running = lax.associative_scan(chain_states, (totals, state))
    entering = jnp.concatenate([jnp.zeros_like(running[1][:1]), running[1][:-1]], axis=0)
    carried = (
        jnp.einsum("cqn,chpn->cqhp", c_blocks.astype(jnp.float32), entering, precision=highest)
        * scaled[..., None]
    )
    return (inner + carried).reshape(sequence_length, head_count, width)


def gated_norm(gated_rows, norm_scale, group_count):
    row_count = gated_rows.shape[0]
    widened = (
        lax.optimization_barrier(gated_rows).astype(jnp.float32).reshape(row_count, group_count, -1)
    )
    power = jnp.mean(widened * widened, axis=-1, keepdims=True)
    return ((widened * lax.rsqrt(power + norm_eps)).reshape(row_count, -1) * norm_scale).astype(
        jnp.bfloat16
    )


def body(query, keys, values, m_x, m_z, m_b, m_c, dt_raw, dt_bias, a_log, d_skip, norm_gain):
    ctx_count = lax.axis_size("ctx")
    context_fold = attend(query, keys, values)
    heads_here = dt_bias.shape[0]
    groups_here = m_b.shape[1] // MN
    per_group = heads_here // groups_here
    rates = jnp.exp(a_log)
    x_cols, z_cols, context_cols = (
        lax.all_to_all(m_x, "ctx", split_axis=1, concat_axis=0, tiled=True),
        lax.all_to_all(m_z, "ctx", split_axis=1, concat_axis=0, tiled=True),
        lax.all_to_all(context_fold, "ctx", split_axis=1, concat_axis=0, tiled=True),
    )
    dt_whole, b_whole, c_whole = (
        lax.all_gather(dt_raw, "ctx", axis=0, tiled=True),
        lax.all_gather(m_b, "ctx", axis=0, tiled=True),
        lax.all_gather(m_c, "ctx", axis=0, tiled=True),
    )
    x_cols = folded_to_sequence(x_cols, ctx_count)
    z_cols = folded_to_sequence(z_cols, ctx_count)
    context_cols = folded_to_sequence(context_cols, ctx_count)
    dt_whole = folded_to_sequence(dt_whole, ctx_count)
    b_whole = folded_to_sequence(b_whole, ctx_count)
    c_whole = folded_to_sequence(c_whole, ctx_count)
    sequence_length = x_cols.shape[0]
    width = x_cols.shape[1]
    sub_width = min(width, MP)
    head_count = width // sub_width
    first_head = lax.axis_index("ctx") * width // MP
    group_index = first_head // per_group
    step_mine = jax.nn.softplus(
        lax.dynamic_slice_in_dim(dt_whole, first_head, head_count, 1).astype(jnp.float32)
        + lax.dynamic_slice_in_dim(dt_bias, first_head, head_count, 0)
    )
    rate_mine = lax.dynamic_slice_in_dim(rates, first_head, head_count, 0)
    skip_mine = lax.dynamic_slice_in_dim(d_skip, first_head, head_count, 0)
    b_mine = lax.dynamic_slice_in_dim(b_whole, group_index * MN, MN, 1)
    c_mine = lax.dynamic_slice_in_dim(c_whole, group_index * MN, MN, 1)
    x_mine = x_cols.reshape(sequence_length, head_count, sub_width)
    outputs = ssd_sequence(x_mine, step_mine, rate_mine, b_mine, c_mine)
    outputs = outputs + skip_mine[None, :, None] * x_mine.astype(jnp.float32)
    gated = (
        outputs.reshape(sequence_length, width) * jax.nn.silu(z_cols.astype(jnp.float32))
    ).astype(jnp.bfloat16)
    gated_rows, context = (
        lax.all_to_all(gated, "ctx", split_axis=0, concat_axis=1, tiled=True),
        lax.all_to_all(context_cols, "ctx", split_axis=0, concat_axis=1, tiled=True),
    )
    mixed = gated_norm(gated_rows, norm_gain, groups_here)
    return (context, mixed)


def solution(mesh):
    in_specs = (
        P(("grp", "ctx"), "hd"),
        P(("grp", "ctx"), "hd"),
        P(("grp", "ctx"), "hd"),
        P(("grp", "ctx"), "hd"),
        P(("grp", "ctx"), "hd"),
        P(("grp", "ctx"), "hd"),
        P(("grp", "ctx"), "hd"),
        P(("grp", "ctx"), "hd"),
        P("hd"),
        P("hd"),
        P("hd"),
        P("hd"),
    )
    out_specs = (P(("grp", "ctx"), "hd"), P(("grp", "ctx"), "hd"))
    return jax.shard_map(body, mesh=mesh, in_specs=in_specs, out_specs=out_specs, check_vma=False)
```

profile of v0, /device:TPU:0, one launch (start us, length us, event | category | flops | bytes accessed | tf_op | source)
XLA Modules:
  0.0 158.5 jit_solution(12240753231804312375)
XLA Ops:
  0.6 15.9 %all_gather.16 = bf16[512,256]{1,0:T(8,128)(2,1)S(1)} all-gather(bf16[128,256]{1,0:T(8,128)(2,1)} %param.14), channel_id=1, replica_groups=mesh['grp'=2,'ctx'=4,'hd'=4] {'ctx'}, dimensions={0}, use_global_device_ids=true | all-gather | bytes 327680 | tf_op jit(solution)/shard_map/all_gather | solution.py:52
  16.7 1.0 copy.67
  17.6 13.3 %all_gather.15 = bf16[512,256]{0,1:T(8,128)(2,1)S(1)} all-gather(bf16[128,256]{0,1:T(8,128)(2,1)S(1)} %copy.67), channel_id=1, replica_groups=mesh['grp'=2,'ctx'=4,'hd'=4] {'ctx'}, dimensions={0}, use_global_device_ids=true | all-gather | bytes 327680 | tf_op jit(solution)/shard_map/all_gather | solution.py:51
  30.9 1.1 reshape.189
  34.0 0.9 copy.72
  34.9 4.2 %all-to-all-start = ((bf16[128,4,256]{2,0,1:T(8,128)(2,1)}), bf16[128,4,256]{2,0,1:T(8,128)(2,1)S(1)}, u32[]{:S(2)}, u32[]{:S(2)}) async-start(bf16[128,4,256]{2,0,1:T(8,128)(2,1)} %copy.72), calls=%async_computation | async-start | bytes 524288 | tf_op jit(solution)/shard_map/all_to_all | solution.py:155
  39.0 13.6 %all_gather.19 = bf16[512,32]{0,1:T(8,128)(2,1)S(1)} all-gather(bf16[128,32]{0,1:T(8,128)(2,1)S(1)} %copy-done.10), channel_id=1, replica_groups=mesh['grp'=2,'ctx'=4,'hd'=4] {'ctx'}, dimensions={0}, use_global_device_ids=true | all-gather | bytes 40960 | tf_op jit(solution)/shard_map/all_gather | solution.py:158
  53.6 14.5 %all_gather.18 = bf16[512,256]{1,0:T(8,128)(2,1)S(1)} all-gather(bf16[128,256]{1,0:T(8,128)(2,1)S(1)} %copy-done.4), channel_id=1, replica_groups=mesh['grp'=2,'ctx'=4,'hd'=4] {'ctx'}, dimensions={0}, use_global_device_ids=true | all-gather | bytes 327680 | tf_op jit(solution)/shard_map/all_gather | solution.py:159
  68.1 14.5 %all_gather.17 = bf16[512,256]{1,0:T(8,128)(2,1)S(1)} all-gather(bf16[128,256]{1,0:T(8,128)(2,1)S(1)} %copy-done.5), channel_id=1, replica_groups=mesh['grp'=2,'ctx'=4,'hd'=4] {'ctx'}, dimensions={0}, use_global_device_ids=true | all-gather | bytes 327680 | tf_op jit(solution)/shard_map/all_gather | solution.py:160
  83.1 0.7 copy.85
  83.8 0.7 copy.83
  84.6 1.0 copy.74
  85.6 1.0 copy.90
  87.6 3.5 %all-to-all-start.2 = ((bf16[128,4,512]{0,2,1:T(8,128)(2,1)}), bf16[128,4,512]{0,2,1:T(8,128)(2,1)S(1)}, u32[]{:S(2)}, u32[]{:S(2)}) async-start(bf16[128,4,512]{0,2,1:T(8,128)(2,1)} %bitcast.18), calls=%async_computation.2 | async-start | bytes 1048576 | tf_op jit(solution)/shard_map/all_to_all | solution.py:153
  91.8 0.9 fusion.61
  92.7 11.7 %all-to-all-done.2 = bf16[128,4,512]{0,2,1:T(8,128)(2,1)S(1)} async-done(((bf16[128,4,512]{0,2,1:T(8,128)(2,1)}), bf16[128,4,512]{0,2,1:T(8,128)(2,1)S(1)}, u32[]{:S(2)}, u32[]{:S(2)}) %all-to-all-start.2) | async-done | bytes 524320 | tf_op jit(solution)/shard_map/all_to_all | solution.py:153
  104.4 3.5 %all-to-all-start.3 = ((bf16[128,4,512]{0,2,1:T(8,128)(2,1)}), bf16[128,4,512]{0,2,1:T(8,128)(2,1)S(1)}, u32[]{:S(2)}, u32[]{:S(2)}) async-start(bf16[128,4,512]{0,2,1:T(8,128)(2,1)} %bitcast.46), calls=%async_computation.3 | async-start | bytes 1048576 | tf_op jit(solution)/shard_map/all_to_all | solution.py:154
  107.9 0.7 pad_maximum_fusion.3
  108.9 10.5 %all-to-all-done.3 = bf16[128,4,512]{0,2,1:T(8,128)(2,1)S(1)} async-done(((bf16[128,4,512]{0,2,1:T(8,128)(2,1)}), bf16[128,4,512]{0,2,1:T(8,128)(2,1)S(1)}, u32[]{:S(2)}, u32[]{:S(2)}) %all-to-all-start.3) | async-done | bytes 524320 | tf_op jit(solution)/shard_map/all_to_all | solution.py:154
  119.5 4.2 %all-to-all-start.1 = ((bf16[4,128,256]{2,1,0:T(8,128)(2,1)}), bf16[4,128,256]{2,1,0:T(8,128)(2,1)}, u32[]{:S(2)}, u32[]{:S(2)}) async-start(bf16[4,128,256]{2,1,0:T(8,128)(2,1)} %bitcast.15), calls=%async_computation.1 | async-start | bytes 524288 | tf_op jit(solution)/shard_map/all_to_all | solution.py:190
  124.0 0.9 pad_maximum_fusion
  126.1 1.8 %fusion = f32[4,8,64,128]{3,2,1,0:T(8,128)S(1)} fusion(bf16[4,128,128,1]{2,1,3,0:T(8,128)(2,1)S(1)} %bitcast.143, f32[4,128,8,64]{3,2,1,0:T(8,128)S(1)} %convert_multiply_fusion), kind=kOutput, calls=%fused_computation.1 | convolution fusion | flops 402653184 | bytes 2228224 | tf_op jit(solution)/shard_map/vmap(jh,jhp,jn->hpn)/dot_general | solution.py:105
  128.1 0.9 pad_add_fusion
  129.3 6.2 %pad.61 = f32[4,8,64,128]{3,2,1,0:T(8,128)S(1)} pad(f32[2,8,64,128]{3,2,1,0:T(8,128)} %pad_add_fusion, f32[]{:T(128)} %constant.92.clone.1), padding=1_0_1x0_0_0x0_0_0x0_0_0 | pad | bytes 1572868
  135.6 0.8 copy-done.3
  136.5 2.7 %fusion.11 = f32[4,128,8,64]{1,3,2,0:T(8,128)S(1)} fusion(bf16[4,128,8,64]{3,2,1,0:T(8,128)(2,1)S(1)} %reshape_reshape_reshape.3, f32[4,128,8]{1,2,0:T(8,128)S(1)} %copy-done.6, f32[4,128,8]{1,2,0:T(8,128)S(1)} %copy-done.7, f32[4,128,128]{2,1,0:T(8,128)S(1)} %copy-done.3, pred[128,128]{1,0:T(8,128)(4,1)S(1)} %copy-done.8), kind=kOutput, calls=%fused_computation.14 | convolution fusion | flops 404750336 | bytes 1884160 | tf_op jit(solution)/shard_map/vmap(ijh,jhp->ihp)/dot_general | solution.py:103
  140.2 1.2 fusion.36
  141.4 5.0 %all-to-all-start.4 = ((bf16[4,128,512]{2,1,0:T(8,128)(2,1)}), bf16[4,128,512]{2,1,0:T(8,128)(2,1)S(1)}, u32[]{:S(2)}, u32[]{:S(2)}) async-start(bf16[4,128,512]{2,1,0:T(8,128)(2,1)} %fusion.36), calls=%async_computation.4 | async-start | bytes 1048576 | tf_op jit(solution)/shard_map/all_to_all | solution.py:189
  146.4 1.1 copy.73
  147.5 0.9 copy.94
  148.4 8.3 %all-to-all-done.4 = bf16[4,128,512]{2,1,0:T(8,128)(2,1)S(1)} async-done(((bf16[4,128,512]{2,1,0:T(8,128)(2,1)}), bf16[4,128,512]{2,1,0:T(8,128)(2,1)S(1)}, u32[]{:S(2)}, u32[]{:S(2)}) %all-to-all-start.4) | async-done | bytes 524320 | tf_op jit(solution)/shard_map/all_to_all | solution.py:189
  157.5 1.0 copy.95
  (96 shorter events, 9.2 us)
Async XLA Ops:
  33.3 5.7 %copy-start.10 = (bf16[128,32]{0,1:T(8,128)(2,1)S(1)}, bf16[128,32]{0,1:T(8,128)(2,1)}, u32[]{:S(2)}) copy-start(bf16[128,32]{0,1:T(8,128)(2,1)} %param.19) | copy-start | bytes 24580
  34.0 19.2 %copy-start.12 = (f32[32]{0:T(128)S(1)}, f32[32]{0:T(128)}, u32[]{:S(2)}) copy-start(f32[32]{0:T(128)} %param.20) | copy-start | bytes 388
  34.0 19.5 %copy-start.13 = (f32[32]{0:T(128)S(1)}, f32[32]{0:T(128)}, u32[]{:S(2)}) copy-start(f32[32]{0:T(128)} %param.21) | copy-start | bytes 388
  34.0 19.6 %copy-start.4 = (bf16[128,256]{1,0:T(8,128)(2,1)S(1)}, bf16[128,256]{1,0:T(8,128)(2,1)}, u32[]{:S(2)}) copy-start(bf16[128,256]{1,0:T(8,128)(2,1)} %param.17) | copy-start | bytes 196612
  34.0 34.1 %copy-start.5 = (bf16[128,256]{1,0:T(8,128)(2,1)S(1)}, bf16[128,256]{1,0:T(8,128)(2,1)}, u32[]{:S(2)}) copy-start(bf16[128,256]{1,0:T(8,128)(2,1)} %param.18) | copy-start | bytes 196612
  34.9 52.8 %all-to-all-start = ((bf16[128,4,256]{2,0,1:T(8,128)(2,1)}), bf16[128,4,256]{2,0,1:T(8,128)(2,1)S(1)}, u32[]{:S(2)}, u32[]{:S(2)}) async-start(bf16[128,4,256]{2,0,1:T(8,128)(2,1)} %copy.72), calls=%async_computation | async-start | bytes 524288 | tf_op jit(solution)/shard_map/all_to_all | solution.py:155
  68.1 16.5 %copy-start.1 = (bf16[128,2048]{1,0:T(8,128)(2,1)S(1)}, bf16[128,2048]{1,0:T(8,128)(2,1)}, u32[]{:S(2)}) copy-start(bf16[128,2048]{1,0:T(8,128)(2,1)} %param.15) | copy-start | bytes 1572868
  82.7 2.9 %copy-start.2 = (bf16[128,2048]{1,0:T(8,128)(2,1)S(1)}, bf16[128,2048]{1,0:T(8,128)(2,1)}, u32[]{:S(2)}) copy-start(bf16[128,2048]{1,0:T(8,128)(2,1)} %param.16) | copy-start | bytes 1572868
  83.0 3.7 %copy-start.14 = (f32[32]{0:T(128)S(1)}, f32[32]{0:T(128)}, u32[]{:S(2)}) copy-start(f32[32]{0:T(128)} %param.22) | copy-start | bytes 388
  87.6 16.7 %all-to-all-start.2 = ((bf16[128,4,512]{0,2,1:T(8,128)(2,1)}), bf16[128,4,512]{0,2,1:T(8,128)(2,1)S(1)}, u32[]{:S(2)}, u32[]{:S(2)}) async-start(bf16[128,4,512]{0,2,1:T(8,128)(2,1)} %bitcast.18), calls=%async_computation.2 | async-start | bytes 1048576 | tf_op jit(solution)/shard_map/all_to_all | solution.py:153
  104.4 15.1 %all-to-all-start.3 = ((bf16[128,4,512]{0,2,1:T(8,128)(2,1)}), bf16[128,4,512]{0,2,1:T(8,128)(2,1)S(1)}, u32[]{:S(2)}, u32[]{:S(2)}) async-start(bf16[128,4,512]{0,2,1:T(8,128)(2,1)} %bitcast.46), calls=%async_computation.3 | async-start | bytes 1048576 | tf_op jit(solution)/shard_map/all_to_all | solution.py:154
  119.5 21.9 %all-to-all-start.1 = ((bf16[4,128,256]{2,1,0:T(8,128)(2,1)}), bf16[4,128,256]{2,1,0:T(8,128)(2,1)}, u32[]{:S(2)}, u32[]{:S(2)}) async-start(bf16[4,128,256]{2,1,0:T(8,128)(2,1)} %bitcast.15), calls=%async_computation.1 | async-start | bytes 524288 | tf_op jit(solution)/shard_map/all_to_all | solution.py:190
  135.5 0.9 copy-start.3
  135.5 1.0 copy-start.6
  135.5 1.0 copy-start.7
  135.5 0.9 copy-start.8
  139.2 1.0 copy-start
  139.2 1.0 copy-start.11
  141.4 15.7 %copy-start.9 = (f32[2048]{0:T(1024)S(1)}, f32[2048]{0:T(1024)}, u32[]{:S(2)}) copy-start(f32[2048]{0:T(1024)} %param.23) | copy-start | bytes 24580
  141.4 15.3 %all-to-all-start.4 = ((bf16[4,128,512]{2,1,0:T(8,128)(2,1)}), bf16[4,128,512]{2,1,0:T(8,128)(2,1)S(1)}, u32[]{:S(2)}, u32[]{:S(2)}) async-start(bf16[4,128,512]{2,1,0:T(8,128)(2,1)} %fusion.36), calls=%async_computation.4 | async-start | bytes 1048576 | tf_op jit(solution)/shard_map/all_to_all | solution.py:189
where the time goes:
time: 160 us; the launch traced here: 158 us
  blocking collectives  71.8 us (45%)
  waiting for transfers between devices  30.6 us (19%)
  local copies, waits for them, and re-layouts  20.3 us (13%)
  starting transfers between devices  20.3 us (13%)
  matrix products  7.27 us (5%)
  other arithmetic  7.03 us (4%)
    all_gather x1, blocking collectives, attend(): value_piece = lax.all_gather(values, 'ctx', axis=0, tiled=True)  15.9 us
    all_gather x1, blocking collectives, body(): lax.all_gather(m_c, 'ctx', axis=0, tiled=True)  14.5 us
    all_gather x1, blocking collectives, body(): lax.all_gather(m_b, 'ctx', axis=0, tiled=True)  14.5 us
    all_gather x1, blocking collectives, body(): lax.all_gather(dt_raw, 'ctx', axis=0, tiled=True)  13.6 us
    all_gather x1, blocking collectives, attend(): key_piece = lax.all_gather(keys, 'ctx', axis=0, tiled=True)  13.3 us
    unnamed x36, local copies, waits for them, and re-layouts  12 us
    all_to_all x1, waiting for transfers between devices, body(): lax.all_to_all(m_x, 'ctx', split_axis=1, concat_axis=0, tiled=True)  11.7 us
    all_to_all x1, waiting for transfers between devices, body(): lax.all_to_all(m_z, 'ctx', split_axis=1, concat_axis=0, tiled=True)  10.5 us
  transfers between devices with their start and end apart: 5, of which 3 were waited for; matrix products, arithmetic and copies ran while one was open for 17% of the time, Pallas kernels for 0%

commit v1 on v0

--- a/solution.py
+++ b/solution.py
@@ -48,8 +48,11 @@
     start_sum = jnp.zeros((kv_local, heads_per_group, tok_rows), jnp.float32)
     start_acc = jnp.zeros((kv_local, heads_per_group, tok_rows, HEAD_SIZE), jnp.float32)
     start = jnp.int32(0)
-    key_piece = lax.all_gather(keys, "ctx", axis=0, tiled=True)
-    value_piece = lax.all_gather(values, "ctx", axis=0, tiled=True)
+    key_piece, value_piece = jnp.split(
+        lax.all_gather(jnp.concatenate([keys, values], axis=1), "ctx", axis=0, tiled=True),
+        [keys.shape[1]],
+        axis=1,
+    )
     piece_rows = key_piece.shape[0]
     rows_per_block = pick_block(piece_rows, 1024)
 

time: 160 us -> 149 us (0.931)
  blocking collectives: 71.8 us -> 58.6 us
  waiting for transfers between devices: 30.6 us -> 33.6 us
    all_gather x2 -> x1, blocking collectives: 29.1 us -> 16.7 us  [attend(): lax.all_gather(jnp.concatenate([keys, values], axis=1), 'ctx', axis=0, ti...]
    all_to_all x1, waiting for transfers between devices: 11.7 us -> 13.3 us  [body(): lax.all_to_all(m_x, 'ctx', split_axis=1, concat_axis=0, tiled=True)]
    unnamed x36 -> x39, local copies, waits for them, and re-layouts: 12 us -> 13 us
  transfers between devices with their start and end apart: 5 -> 5, of which waited for: 3 -> 3; matrix products, arithmetic and copies ran while one was open for 17% -> 18% of each run, Pallas kernels for 0% -> 0%
where the time goes in v1:
time: 149 us; the launch traced here: 148 us
  blocking collectives  58.6 us (39%)
  waiting for transfers between devices  33.6 us (23%)
  local copies, waits for them, and re-layouts  20.2 us (14%)
  starting transfers between devices  19.8 us (13%)
  matrix products  7.28 us (5%)
  other arithmetic  7.04 us (5%)
    all_gather x1, blocking collectives, attend(): lax.all_gather(jnp.concatenate([keys, values], axis=1), 'ctx', axis=0, ti...  16.7 us
    all_gather x1, blocking collectives, body(): lax.all_gather(m_b, 'ctx', axis=0, tiled=True)  14.2 us
    all_gather x1, blocking collectives, body(): lax.all_gather(m_c, 'ctx', axis=0, tiled=True)  13.9 us
    all_gather x1, blocking collectives, body(): lax.all_gather(dt_raw, 'ctx', axis=0, tiled=True)  13.7 us
    all_to_all x1, waiting for transfers between devices, body(): lax.all_to_all(m_x, 'ctx', split_axis=1, concat_axis=0, tiled=True)  13.3 us
    unnamed x39, local copies, waits for them, and re-layouts  13 us
    all_to_all x1, waiting for transfers between devices, body(): lax.all_to_all(m_z, 'ctx', split_axis=1, concat_axis=0, tiled=True)  12 us
    all_to_all x1, waiting for transfers between devices, body(): lax.all_to_all(gated, 'ctx', split_axis=0, concat_axis=1, tiled=True)  8.31 us
  transfers between devices with their start and end apart: 5, of which 3 were waited for; matrix products, arithmetic and copies ran while one was open for 18% of the time, Pallas kernels for 0%

profile of v1, /device:TPU:0, one launch (start us, length us, event | category | flops | bytes accessed | tf_op | source)
XLA Modules:
  0.0 147.7 jit_solution(5453998042836031995)
XLA Ops:
  0.7 1.0 copy.68
  1.7 1.0 copy.67
  2.6 16.7 %all_gather.12 = bf16[512,512]{0,1:T(8,128)(2,1)S(1)} all-gather(bf16[128,512]{0,1:T(8,128)(2,1)S(1)} %pad_maximum_fusion.6), channel_id=1, replica_groups=mesh['grp'=2,'ctx'=4,'hd'=4] {'ctx'}, dimensions={0}, use_global_device_ids=true | all-gather | bytes 655360 | tf_op jit(solution)/shard_map/all_gather | solution.py:52
  20.9 0.7 fusion.17
  21.6 0.9 copy.72
  22.4 3.7 %all-to-all-start = ((bf16[128,4,256]{2,0,1:T(8,128)(2,1)}), bf16[128,4,256]{2,0,1:T(8,128)(2,1)S(1)}, u32[]{:S(2)}, u32[]{:S(2)}) async-start(bf16[128,4,256]{2,0,1:T(8,128)(2,1)} %copy.72), calls=%async_computation | async-start | bytes 524288 | tf_op jit(solution)/shard_map/all_to_all | solution.py:158
  26.1 13.7 %all_gather.15 = bf16[512,32]{0,1:T(8,128)(2,1)S(1)} all-gather(bf16[128,32]{0,1:T(8,128)(2,1)S(1)} %copy-done.11), channel_id=1, replica_groups=mesh['grp'=2,'ctx'=4,'hd'=4] {'ctx'}, dimensions={0}, use_global_device_ids=true | all-gather | bytes 40960 | tf_op jit(solution)/shard_map/all_gather | solution.py:161
  40.7 14.2 %all_gather.14 = bf16[512,256]{1,0:T(8,128)(2,1)S(1)} all-gather(bf16[128,256]{1,0:T(8,128)(2,1)S(1)} %copy-done.5), channel_id=1, replica_groups=mesh['grp'=2,'ctx'=4,'hd'=4] {'ctx'}, dimensions={0}, use_global_device_ids=true | all-gather | bytes 327680 | tf_op jit(solution)/shard_map/all_gather | solution.py:162
  55.0 13.9 %all_gather.13 = bf16[512,256]{1,0:T(8,128)(2,1)S(1)} all-gather(bf16[128,256]{1,0:T(8,128)(2,1)S(1)} %copy-done.6), channel_id=1, replica_groups=mesh['grp'=2,'ctx'=4,'hd'=4] {'ctx'}, dimensions={0}, use_global_device_ids=true | all-gather | bytes 327680 | tf_op jit(solution)/shard_map/all_gather | solution.py:163
  69.3 0.7 copy.85
  70.1 0.7 copy.83
  70.8 1.0 copy.74
  71.8 1.0 copy.90
  73.9 3.5 %all-to-all-start.2 = ((bf16[128,4,512]{0,2,1:T(8,128)(2,1)}), bf16[128,4,512]{0,2,1:T(8,128)(2,1)S(1)}, u32[]{:S(2)}, u32[]{:S(2)}) async-start(bf16[128,4,512]{0,2,1:T(8,128)(2,1)} %bitcast.18), calls=%async_computation.2 | async-start | bytes 1048576 | tf_op jit(solution)/shard_map/all_to_all | solution.py:156
  78.0 0.9 fusion.62
  78.9 13.3 %all-to-all-done.2 = bf16[128,4,512]{0,2,1:T(8,128)(2,1)S(1)} async-done(((bf16[128,4,512]{0,2,1:T(8,128)(2,1)}), bf16[128,4,512]{0,2,1:T(8,128)(2,1)S(1)}, u32[]{:S(2)}, u32[]{:S(2)}) %all-to-all-start.2) | async-done | bytes 524320 | tf_op jit(solution)/shard_map/all_to_all | solution.py:156
  92.2 3.5 %all-to-all-start.3 = ((bf16[128,4,512]{0,2,1:T(8,128)(2,1)}), bf16[128,4,512]{0,2,1:T(8,128)(2,1)S(1)}, u32[]{:S(2)}, u32[]{:S(2)}) async-start(bf16[128,4,512]{0,2,1:T(8,128)(2,1)} %bitcast.46), calls=%async_computation.3 | async-start | bytes 1048576 | tf_op jit(solution)/shard_map/all_to_all | solution.py:157
  95.7 0.7 pad_maximum_fusion.3
  96.8 12.0 %all-to-all-done.3 = bf16[128,4,512]{0,2,1:T(8,128)(2,1)S(1)} async-done(((bf16[128,4,512]{0,2,1:T(8,128)(2,1)}), bf16[128,4,512]{0,2,1:T(8,128)(2,1)S(1)}, u32[]{:S(2)}, u32[]{:S(2)}) %all-to-all-start.3) | async-done | bytes 524320 | tf_op jit(solution)/shard_map/all_to_all | solution.py:157
  108.8 4.2 %all-to-all-start.1 = ((bf16[4,128,256]{2,1,0:T(8,128)(2,1)}), bf16[4,128,256]{2,1,0:T(8,128)(2,1)}, u32[]{:S(2)}, u32[]{:S(2)}) async-start(bf16[4,128,256]{2,1,0:T(8,128)(2,1)} %bitcast.15), calls=%async_computation.1 | async-start | bytes 524288 | tf_op jit(solution)/shard_map/all_to_all | solution.py:193
  113.3 0.9 pad_maximum_fusion
  115.3 1.8 %fusion = f32[4,8,64,128]{3,2,1,0:T(8,128)S(1)} fusion(bf16[4,128,128,1]{2,1,3,0:T(8,128)(2,1)S(1)} %bitcast.143, f32[4,128,8,64]{3,2,1,0:T(8,128)S(1)} %convert_multiply_fusion), kind=kOutput, calls=%fused_computation.1 | convolution fusion | flops 402653184 | bytes 2228224 | tf_op jit(solution)/shard_map/vmap(jh,jhp,jn->hpn)/dot_general | solution.py:108
  117.3 0.9 pad_add_fusion
  118.5 6.2 %pad.65 = f32[4,8,64,128]{3,2,1,0:T(8,128)S(1)} pad(f32[2,8,64,128]{3,2,1,0:T(8,128)} %pad_add_fusion, f32[]{:T(128)} %constant.92.clone.1), padding=1_0_1x0_0_0x0_0_0x0_0_0 | pad | bytes 1572868
  124.9 0.8 copy-done.4
  125.7 2.7 %fusion.11 = f32[4,128,8,64]{1,3,2,0:T(8,128)S(1)} fusion(bf16[4,128,8,64]{3,2,1,0:T(8,128)(2,1)S(1)} %reshape_reshape_reshape.3, f32[4,128,8]{1,2,0:T(8,128)S(1)} %copy-done.7, f32[4,128,8]{1,2,0:T(8,128)S(1)} %copy-done.8, f32[4,128,128]{2,1,0:T(8,128)S(1)} %copy-done.4, pred[128,128]{1,0:T(8,128)(4,1)S(1)} %copy-done.9), kind=kOutput, calls=%fused_computation.14 | convolution fusion | flops 404750336 | bytes 1884160 | tf_op jit(solution)/shard_map/vmap(ijh,jhp->ihp)/dot_general | solution.py:106
  129.5 1.2 fusion.36
  130.6 5.0 %all-to-all-start.4 = ((bf16[4,128,512]{2,1,0:T(8,128)(2,1)}), bf16[4,128,512]{2,1,0:T(8,128)(2,1)S(1)}, u32[]{:S(2)}, u32[]{:S(2)}) async-start(bf16[4,128,512]{2,1,0:T(8,128)(2,1)} %fusion.36), calls=%async_computation.4 | async-start | bytes 1048576 | tf_op jit(solution)/shard_map/all_to_all | solution.py:192
  135.6 1.1 copy.73
  136.8 0.9 copy.94
  137.6 8.3 %all-to-all-done.4 = bf16[4,128,512]{2,1,0:T(8,128)(2,1)S(1)} async-done(((bf16[4,128,512]{2,1,0:T(8,128)(2,1)}), bf16[4,128,512]{2,1,0:T(8,128)(2,1)S(1)}, u32[]{:S(2)}, u32[]{:S(2)}) %all-to-all-start.4) | async-done | bytes 524320 | tf_op jit(solution)/shard_map/all_to_all | solution.py:192
  146.7 1.0 copy.95
  (99 shorter events, 8.6 us)
Async XLA Ops:
  0.6 18.8 %copy-start.3 = (bf16[128,1024]{1,0:T(8,128)(2,1)S(1)}, bf16[128,1024]{1,0:T(8,128)(2,1)}, u32[]{:S(2)}) copy-start(bf16[128,1024]{1,0:T(8,128)(2,1)} %param.12) | copy-start | bytes 786436
  20.8 5.2 %copy-start.11 = (bf16[128,32]{0,1:T(8,128)(2,1)S(1)}, bf16[128,32]{0,1:T(8,128)(2,1)}, u32[]{:S(2)}) copy-start(bf16[128,32]{0,1:T(8,128)(2,1)} %param.19) | copy-start | bytes 24580
  21.5 18.8 %copy-start.13 = (f32[32]{0:T(128)S(1)}, f32[32]{0:T(128)}, u32[]{:S(2)}) copy-start(f32[32]{0:T(128)} %param.20) | copy-start | bytes 388
  21.5 19.1 %copy-start.14 = (f32[32]{0:T(128)S(1)}, f32[32]{0:T(128)}, u32[]{:S(2)}) copy-start(f32[32]{0:T(128)} %param.21) | copy-start | bytes 388
  21.6 19.1 %copy-start.5 = (bf16[128,256]{1,0:T(8,128)(2,1)S(1)}, bf16[128,256]{1,0:T(8,128)(2,1)}, u32[]{:S(2)}) copy-start(bf16[128,256]{1,0:T(8,128)(2,1)} %param.17) | copy-start | bytes 196612
  21.6 33.4 %copy-start.6 = (bf16[128,256]{1,0:T(8,128)(2,1)S(1)}, bf16[128,256]{1,0:T(8,128)(2,1)}, u32[]{:S(2)}) copy-start(bf16[128,256]{1,0:T(8,128)(2,1)} %param.18) | copy-start | bytes 196612
  22.4 51.4 %all-to-all-start = ((bf16[128,4,256]{2,0,1:T(8,128)(2,1)}), bf16[128,4,256]{2,0,1:T(8,128)(2,1)S(1)}, u32[]{:S(2)}, u32[]{:S(2)}) async-start(bf16[128,4,256]{2,0,1:T(8,128)(2,1)} %copy.72), calls=%async_computation | async-start | bytes 524288 | tf_op jit(solution)/shard_map/all_to_all | solution.py:158
  54.9 15.9 %copy-start.1 = (bf16[128,2048]{1,0:T(8,128)(2,1)S(1)}, bf16[128,2048]{1,0:T(8,128)(2,1)}, u32[]{:S(2)}) copy-start(bf16[128,2048]{1,0:T(8,128)(2,1)} %param.15) | copy-start | bytes 1572868
  68.9 2.9 %copy-start.2 = (bf16[128,2048]{1,0:T(8,128)(2,1)S(1)}, bf16[128,2048]{1,0:T(8,128)(2,1)}, u32[]{:S(2)}) copy-start(bf16[128,2048]{1,0:T(8,128)(2,1)} %param.16) | copy-start | bytes 1572868
  69.2 3.7 %copy-start.15 = (f32[32]{0:T(128)S(1)}, f32[32]{0:T(128)}, u32[]{:S(2)}) copy-start(f32[32]{0:T(128)} %param.22) | copy-start | bytes 388
  73.9 18.4 %all-to-all-start.2 = ((bf16[128,4,512]{0,2,1:T(8,128)(2,1)}), bf16[128,4,512]{0,2,1:T(8,128)(2,1)S(1)}, u32[]{:S(2)}, u32[]{:S(2)}) async-start(bf16[128,4,512]{0,2,1:T(8,128)(2,1)} %bitcast.18), calls=%async_computation.2 | async-start | bytes 1048576 | tf_op jit(solution)/shard_map/all_to_all | solution.py:156
  92.2 16.5 %all-to-all-start.3 = ((bf16[128,4,512]{0,2,1:T(8,128)(2,1)}), bf16[128,4,512]{0,2,1:T(8,128)(2,1)S(1)}, u32[]{:S(2)}, u32[]{:S(2)}) async-start(bf16[128,4,512]{0,2,1:T(8,128)(2,1)} %bitcast.46), calls=%async_computation.3 | async-start | bytes 1048576 | tf_op jit(solution)/shard_map/all_to_all | solution.py:157
  108.8 21.9 %all-to-all-start.1 = ((bf16[4,128,256]{2,1,0:T(8,128)(2,1)}), bf16[4,128,256]{2,1,0:T(8,128)(2,1)}, u32[]{:S(2)}, u32[]{:S(2)}) async-start(bf16[4,128,256]{2,1,0:T(8,128)(2,1)} %bitcast.15), calls=%async_computation.1 | async-start | bytes 524288 | tf_op jit(solution)/shard_map/all_to_all | solution.py:193
  124.7 0.9 copy-start.4
  124.8 1.0 copy-start.7
  124.8 1.0 copy-start.8
  124.8 0.9 copy-start.9
  128.4 1.0 copy-start
  128.4 1.0 copy-start.12
  130.6 15.7 %copy-start.10 = (f32[2048]{0:T(1024)S(1)}, f32[2048]{0:T(1024)}, u32[]{:S(2)}) copy-start(f32[2048]{0:T(1024)} %param.23) | copy-start | bytes 24580
  130.6 15.3 %all-to-all-start.4 = ((bf16[4,128,512]{2,1,0:T(8,128)(2,1)}), bf16[4,128,512]{2,1,0:T(8,128)(2,1)S(1)}, u32[]{:S(2)}, u32[]{:S(2)}) async-start(bf16[4,128,512]{2,1,0:T(8,128)(2,1)} %fusion.36), calls=%async_computation.4 | async-start | bytes 1048576 | tf_op jit(solution)/shard_map/all_to_all | solution.py:192
